TPU v7x, 32 devices: a whole 2x2x4 slice. The times are simulated.
32 devices in a mesh: groups: 2 (over y), rows: 4 (over z), cols: 2 (over x), sub: 2 (over core).
Axes of the slice: x: 2, y: 2, z: 4, core: 2. Of those that a mesh axis runs over, the one named last changes fastest.
Arguments:
- returns: float32 [8, 64, 8192], P('groups', 'rows', ('cols', 'sub')), parts along dimension 0, may hold values from -6 to 6
- starts: int32 [8, 8192], P('groups', ('cols', 'sub')), parts along dimension 0, may hold values from 0 to 32
- start_block: float32 [8, 32, 8192], P('groups', None, ('cols', 'sub')), parts along dimension 0, may hold values from -6 to 6
Outputs:
- loadings: float32 [8, 32, 8192], P('groups', None, ('cols', 'sub')), parts along dimension 0
There are 2 independent parts, one for each index of `groups`. A program takes and returns all parts, laid end to end along the dimension named above; each array names one. Nothing has to cross between parts.
Inputs may be any that keep to these rules, and one draw needn't show every extreme that they name: `starts`: days before an asset's start day hold returns that do not count.
All inputs are finite; a program needn't handle non-finite values.
Results may differ from a plain program's by a relative error of at most 0.0078.
Values may be sent and summed in bfloat16 or wider, within the bound.
A program may use at most 64 MiB of HBM per device.

v0:
```python
import jax
import jax.numpy as jnp
from jax import lax
from jax.sharding import PartitionSpec as P

ASSETS = 8192
ITERS = 3


def gram_of(image):
    return jnp.einsum("wkj,wlj->wkl", image, image, precision=lax.Precision.HIGHEST)


def project(factors, scaled):
    rounded = factors.astype(jnp.bfloat16)
    return jnp.einsum("wka,wta->wkt", rounded, scaled, preferred_element_type=jnp.float32)


def expand(proj, widened):
    return jnp.einsum("wkt,wta->wka", proj, widened, precision=lax.Precision.HIGHEST)


def orthonormal(image, gram):
    lower = jnp.linalg.cholesky(gram / ASSETS)
    return jax.scipy.linalg.solve_triangular(lower, image, lower=True)


def on_device(returns, starts, start_block):
    windows, days, width = returns.shape
    rows_count = lax.axis_size("rows")
    row_pos = lax.axis_index("rows")
    total_days = days * rows_count
    day_index = row_pos * days + jnp.arange(days, dtype=jnp.int32)
    live = (day_index[None, :, None] >= starts[:, None, :]).astype(jnp.float32)
    counts = (total_days - starts).astype(jnp.float32)
    masked = live * returns
    sums = lax.psum(jnp.sum(masked, axis=1), "rows")
    mean = sums / counts
    centered = live * (returns - mean[:, None, :])
    squares = lax.psum(jnp.sum(centered * centered, axis=1), "rows")
    scaled = (centered * lax.rsqrt(squares + 1.0)[:, None, :]).astype(jnp.bfloat16)
    widened = scaled.astype(jnp.float32)
    factors = start_block
    for step in range(ITERS):
        proj = lax.psum(project(factors, scaled), ("cols", "sub"))
        image = lax.psum(expand(proj, widened), "rows")
        gram = lax.psum(gram_of(image), ("cols", "sub"))
        factors = orthonormal(image, gram)
    return factors


def solution(mesh):
    placed = (
        P("groups", "rows", ("cols", "sub")),
        P("groups", ("cols", "sub")),
        P("groups", None, ("cols", "sub")),
    )
    return jax.shard_map(
        on_device,
        mesh=mesh,
        in_specs=placed,
        out_specs=P("groups", None, ("cols", "sub")),
        check_vma=False,
    )
```

profile of v0, /device:TPU:0, one launch (start us, length us, event | category | flops | bytes accessed | tf_op | source)
XLA Modules:
  0.0 354.8 jit_solution(6312155068273593770)
XLA Ops:
  7.9 20.9 %psum.77 = f32[4,2048]{1,0:T(4,128)S(1)} all-reduce(f32[4,2048]{1,0:T(4,128)S(1)} %fusion), channel_id=1, replica_groups=mesh['groups'=2,'rows'=4,'cols'=2,'sub'=2] {'rows'}, use_global_device_ids=true, to_apply=%region_1.0 | all-reduce | flops 8192 | bytes 65536 | tf_op jit(solution)/shard_map/psum | solution.py:37
  29.1 15.8 %psum.78 = f32[4,2048]{1,0:T(4,128)S(1)} all-reduce(f32[4,2048]{1,0:T(4,128)S(1)} %multiply_reduce_fusion), channel_id=1, replica_groups=mesh['groups'=2,'rows'=4,'cols'=2,'sub'=2] {'rows'}, use_global_device_ids=true, to_apply=%region_3.0 | all-reduce | flops 8192 | bytes 65536 | tf_op jit(solution)/shard_map/psum | solution.py:40
  45.3 10.3 %psum.79 = f32[4,32,16]{1,2,0:T(8,128)S(1)} all-reduce(f32[4,32,16]{1,2,0:T(8,128)S(1)} %convolution_bitcast_fusion), channel_id=1, replica_groups=mesh['groups'=2,'rows'=4,'cols'=2,'sub'=2] {'cols','sub'}, use_global_device_ids=true, to_apply=%region_4.0 | all-reduce | flops 2048 | bytes 16384 | tf_op jit(solution)/shard_map/psum | solution.py:45
  55.6 1.6 fusion.9
  57.3 51.6 %all-reduce.4.cloned.1.call-done = f32[4,32,2048]{2,1,0:T(8,128)} async-done(((f32[4,32,2048]{2,1,0:T(8,128)}), f32[4,32,2048]{2,1,0:T(8,128)}) %all-reduce.4.cloned.1.call-update) | async-done | bytes 1048592 | tf_op jit(solution)/shard_map/psum | solution.py:46
  108.8 2.7 fusion.10
  111.6 11.8 %psum.81 = f32[4,32,32]{1,2,0:T(8,128)S(1)} all-reduce(f32[4,32,32]{1,2,0:T(8,128)S(1)} %fusion.10), channel_id=1, replica_groups=mesh['groups'=2,'rows'=4,'cols'=2,'sub'=2] {'cols','sub'}, use_global_device_ids=true, to_apply=%region_6.0 | all-reduce | flops 4096 | bytes 32768 | tf_op jit(solution)/shard_map/psum | solution.py:47
  123.6 11.7 %custom-call.10 = f32[4,32,32]{2,1,0:T(8,128)S(1)} custom-call(f32[4,32,32]{2,1,0:T(8,128)S(1)} %fusion.8), custom_call_target="Cholesky" | custom-call | tf_op jit(solution)/shard_map/jit(cholesky)/cholesky | solution.py:24
  135.5 9.8 %custom-call.11 = f32[4,1,32,32]{2,3,1,0:T(8,128)S(1)} custom-call(f32[4,1,32,32]{3,2,1,0:T(8,128)S(1)} %select_bitcast_fusion.2), custom_call_target="InvertDiagBlocksLowerTriangular" | custom-call | tf_op jit(solution)/shard_map/jit(_solve_triangular)/vmap()/triangular_solve | solution.py:25
  146.7 10.5 %psum.82 = f32[4,32,16]{1,2,0:T(8,128)S(1)} all-reduce(f32[4,32,16]{1,2,0:T(8,128)S(1)} %fusion.11), channel_id=1, replica_groups=mesh['groups'=2,'rows'=4,'cols'=2,'sub'=2] {'cols','sub'}, use_global_device_ids=true, to_apply=%region_9.0 | all-reduce | flops 2048 | bytes 16384 | tf_op jit(solution)/shard_map/psum | solution.py:45
  157.2 1.6 fusion.12
  158.8 50.5 %all-reduce.6.cloned.1.call-done = f32[4,32,2048]{2,1,0:T(8,128)} async-done(((f32[4,32,2048]{2,1,0:T(8,128)}), f32[4,32,2048]{2,1,0:T(8,128)}) %all-reduce.6.cloned.1.call-update) | async-done | bytes 1048592 | tf_op jit(solution)/shard_map/psum | solution.py:46
  209.3 2.7 fusion.13
  212.0 11.8 %psum.84 = f32[4,32,32]{1,2,0:T(8,128)S(1)} all-reduce(f32[4,32,32]{1,2,0:T(8,128)S(1)} %fusion.13), channel_id=1, replica_groups=mesh['groups'=2,'rows'=4,'cols'=2,'sub'=2] {'cols','sub'}, use_global_device_ids=true, to_apply=%region_11.0 | all-reduce | flops 4096 | bytes 32768 | tf_op jit(solution)/shard_map/psum | solution.py:47
  224.0 11.7 %custom-call.12 = f32[4,32,32]{2,1,0:T(8,128)S(1)} custom-call(f32[4,32,32]{2,1,0:T(8,128)S(1)} %fusion.6), custom_call_target="Cholesky" | custom-call | tf_op jit(solution)/shard_map/jit(cholesky)/cholesky | solution.py:24
  236.0 9.8 %custom-call.13 = f32[4,1,32,32]{2,3,1,0:T(8,128)S(1)} custom-call(f32[4,1,32,32]{3,2,1,0:T(8,128)S(1)} %select_bitcast_fusion.1), custom_call_target="InvertDiagBlocksLowerTriangular" | custom-call | tf_op jit(solution)/shard_map/jit(_solve_triangular)/vmap()/triangular_solve | solution.py:25
  247.1 10.5 %psum.85 = f32[4,32,16]{1,2,0:T(8,128)S(1)} all-reduce(f32[4,32,16]{1,2,0:T(8,128)S(1)} %fusion.14), channel_id=1, replica_groups=mesh['groups'=2,'rows'=4,'cols'=2,'sub'=2] {'cols','sub'}, use_global_device_ids=true, to_apply=%region_12.0 | all-reduce | flops 2048 | bytes 16384 | tf_op jit(solution)/shard_map/psum | solution.py:45
  257.6 1.6 fusion.15
  259.2 50.5 %all-reduce.8.cloned.1.call-done = f32[4,32,2048]{2,1,0:T(8,128)} async-done(((f32[4,32,2048]{2,1,0:T(8,128)}), f32[4,32,2048]{2,1,0:T(8,128)}) %all-reduce.8.cloned.1.call-update) | async-done | bytes 1048592 | tf_op jit(solution)/shard_map/psum | solution.py:46
  309.7 2.7 fusion.16
  312.5 11.8 %psum.87 = f32[4,32,32]{1,2,0:T(8,128)S(1)} all-reduce(f32[4,32,32]{1,2,0:T(8,128)S(1)} %fusion.16), channel_id=1, replica_groups=mesh['groups'=2,'rows'=4,'cols'=2,'sub'=2] {'cols','sub'}, use_global_device_ids=true, to_apply=%region_14.17 | all-reduce | flops 4096 | bytes 32768 | tf_op jit(solution)/shard_map/psum | solution.py:47
  324.5 11.7 %custom-call.14 = f32[4,32,32]{2,1,0:T(8,128)S(1)} custom-call(f32[4,32,32]{2,1,0:T(8,128)S(1)} %fusion.4), custom_call_target="Cholesky" | custom-call | tf_op jit(solution)/shard_map/jit(cholesky)/cholesky | solution.py:24
  336.4 9.8 %custom-call.15 = f32[4,1,32,32]{2,3,1,0:T(8,128)S(1)} custom-call(f32[4,1,32,32]{3,2,1,0:T(8,128)S(1)} %select_bitcast_fusion), custom_call_target="InvertDiagBlocksLowerTriangular" | custom-call | tf_op jit(solution)/shard_map/jit(_solve_triangular)/vmap()/triangular_solve | solution.py:25
  346.3 2.0 fusion.2
  (49 shorter events, 5.8 us)
Async XLA Ops:
  6.5 22.3 %copy-start.3 = (f32[4,16,2048]{2,1,0:T(8,128)S(1)}, f32[4,16,2048]{2,1,0:T(8,128)}, u32[]{:S(2)}) copy-start(f32[4,16,2048]{2,1,0:T(8,128)} %param.6) | copy-start | bytes 1572868
  6.5 102.3 %all-reduce.4.cloned.1.call-start = ((), (), s32[]{:S(2)}) async-start(), calls=%async_computation | async-start | bytes 2097152 | tf_op jit(solution)/shard_map/psum | solution.py:46
  6.5 22.3 %copy-start.5 = (s32[4,2048]{1,0:T(4,128)S(1)}, s32[4,2048]{1,0:T(4,128)}, u32[]{:S(2)}) copy-start(s32[4,2048]{1,0:T(4,128)} %param.7) | copy-start | bytes 98308
  7.8 37.2 %copy-start.4 = (f32[4,32,2048]{2,1,0:T(8,128)S(1)}, f32[4,32,2048]{2,1,0:T(8,128)}, u32[]{:S(2)}) copy-start(f32[4,32,2048]{2,1,0:T(8,128)} %param.8) | copy-start | bytes 3145732
  57.2 152.1 %all-reduce.6.cloned.1.call-start = ((), (), s32[]{:S(2)}) async-start(), calls=%async_computation.1 | async-start | bytes 2097152 | tf_op jit(solution)/shard_map/psum | solution.py:46
  108.8 36.5 %copy-start = (f32[4,32,2048]{2,1,0:T(8,128)S(1)}, f32[4,32,2048]{2,1,0:T(8,128)}, u32[]{:S(2)}) copy-start(f32[4,32,2048]{2,1,0:T(8,128)} %all-reduce.4.cloned.1.call-done) | copy-start | bytes 3145732
  158.8 151.0 %all-reduce.8.cloned.1.call-start = ((), (), s32[]{:S(2)}) async-start(), calls=%async_computation.2 | async-start | bytes 2097152 | tf_op jit(solution)/shard_map/psum | solution.py:46
  209.3 36.5 %copy-start.1 = (f32[4,32,2048]{2,1,0:T(8,128)S(1)}, f32[4,32,2048]{2,1,0:T(8,128)}, u32[]{:S(2)}) copy-start(f32[4,32,2048]{2,1,0:T(8,128)} %all-reduce.6.cloned.1.call-done) | copy-start | bytes 3145732
  309.7 36.5 %copy-start.2 = (f32[4,32,2048]{2,1,0:T(8,128)S(1)}, f32[4,32,2048]{2,1,0:T(8,128)}, u32[]{:S(2)}) copy-start(f32[4,32,2048]{2,1,0:T(8,128)} %all-reduce.8.cloned.1.call-done) | copy-start | bytes 3145732
Sparse Core Ops, SparseCore 0:
  57.3 51.4 all-reduce.3
  158.9 50.3 all-reduce.5
  259.3 50.3 all-reduce.7
where the time goes:
time: 355 us
  waiting for transfers between devices  153 us (43%)
  blocking collectives  103 us (29%)
  other arithmetic  67.2 us (19%)
  matrix products  17.9 us (5%)
  between operations  13.4 us (4%)
    psum x3, waiting for transfers between devices, on_device(): image = lax.psum(expand(proj, widened), 'rows')  153 us
    another operation x10, other arithmetic, orthonormal(): lower = jnp.linalg.cholesky(gram / ASSETS)  35.6 us
    psum x3, blocking collectives, on_device(): gram = lax.psum(gram_of(image), ('cols', 'sub'))  35.5 us
    psum x3, blocking collectives, on_device(): proj = lax.psum(project(factors, scaled), ('cols', 'sub'))  31.2 us
    another operation x7, other arithmetic, orthonormal(): return jax.scipy.linalg.solve_triangular(lower, image, lower=True)  29.8 us
    psum x1, blocking collectives, on_device(): sums = lax.psum(jnp.sum(masked, axis=1), 'rows')  20.9 us
    psum x1, blocking collectives, on_device(): squares = lax.psum(jnp.sum(centered * centered, axis=1), 'rows')  15.8 us
    dot_general x3, matrix products, gram_of(): jnp.einsum('wkj,wlj->wkl', image, image, precision=lax.Precision.HIGHEST)  8.19 us
  transfers between devices with their start and end apart: 3, of which 3 were waited for; matrix products, arithmetic and copies ran while one was open for 0% of the time, Pallas kernels for 0%

commit v1 on v0

--- a/solution.py
+++ b/solution.py
@@ -2,6 +2,7 @@
 import jax.numpy as jnp
 from jax import lax
 from jax.sharding import PartitionSpec as P
+from jax.lax import all_gather
 
 ASSETS = 8192
 ITERS = 3
@@ -42,7 +43,11 @@
     widened = scaled.astype(jnp.float32)
     factors = start_block
     for step in range(ITERS):
-        proj = lax.psum(project(factors, scaled), ("cols", "sub"))
+
+        def series_all_meet(v0):
+            return jnp.sum(all_gather(v0, ("cols", "sub")), 0)
+
+        proj = series_all_meet(project(factors, scaled))
         image = lax.psum(expand(proj, widened), "rows")
         gram = lax.psum(gram_of(image), ("cols", "sub"))
         factors = orthonormal(image, gram)

time: 355 us -> 340 us (0.958)
  blocking collectives: 103 us -> 88.5 us
    psum x3 -> x0, blocking collectives: 31.2 us -> none  [on_device(): proj = lax.psum(project(factors, scaled), ('cols', 'sub'))]
    all_gather x0 -> x3, blocking collectives: none -> 16.3 us  [series_all_meet(): return jnp.sum(all_gather(v0, ('cols', 'sub')), 0)]
where the time goes in v1:
time: 340 us
  waiting for transfers between devices  152 us (45%)
  blocking collectives  88.5 us (26%)
  other arithmetic  67.2 us (20%)
  matrix products  17.9 us (5%)
  between operations  13.3 us (4%)
    psum x3, waiting for transfers between devices, on_device(): image = lax.psum(expand(proj, widened), 'rows')  152 us
    another operation x10, other arithmetic, orthonormal(): lower = jnp.linalg.cholesky(gram / ASSETS)  35.6 us
    psum x3, blocking collectives, on_device(): gram = lax.psum(gram_of(image), ('cols', 'sub'))  35.5 us
    another operation x7, other arithmetic, orthonormal(): return jax.scipy.linalg.solve_triangular(lower, image, lower=True)  29.8 us
    psum x1, blocking collectives, on_device(): sums = lax.psum(jnp.sum(masked, axis=1), 'rows')  20.9 us
    all_gather x3, blocking collectives, series_all_meet(): return jnp.sum(all_gather(v0, ('cols', 'sub')), 0)  16.3 us
    psum x1, blocking collectives, on_device(): squares = lax.psum(jnp.sum(centered * centered, axis=1), 'rows')  15.8 us
    dot_general x3, matrix products, gram_of(): jnp.einsum('wkj,wlj->wkl', image, image, precision=lax.Precision.HIGHEST)  8.19 us
  transfers between devices with their start and end apart: 3, of which 3 were waited for; matrix products, arithmetic and copies ran while one was open for 0% of the time, Pallas kernels for 0%

profile of v1, /device:TPU:0, one launch (start us, length us, event | category | flops | bytes accessed | tf_op | source)
XLA Modules:
  0.0 339.6 jit_solution(6191245718169102917)
XLA Ops:
  7.9 20.9 %psum.56 = f32[4,2048]{1,0:T(4,128)S(1)} all-reduce(f32[4,2048]{1,0:T(4,128)S(1)} %fusion), channel_id=1, replica_groups=mesh['groups'=2,'rows'=4,'cols'=2,'sub'=2] {'rows'}, use_global_device_ids=true, to_apply=%region_1.0 | all-reduce | flops 8192 | bytes 65536 | tf_op jit(solution)/shard_map/psum | solution.py:38
  29.1 15.8 %psum.57 = f32[4,2048]{1,0:T(4,128)S(1)} all-reduce(f32[4,2048]{1,0:T(4,128)S(1)} %multiply_reduce_fusion), channel_id=1, replica_groups=mesh['groups'=2,'rows'=4,'cols'=2,'sub'=2] {'rows'}, use_global_device_ids=true, to_apply=%region_3.0 | all-reduce | flops 8192 | bytes 65536 | tf_op jit(solution)/shard_map/psum | solution.py:41
  45.3 5.4 %all-gather = f32[16,32,16]{1,2,0:T(8,128)S(1)} all-gather(f32[4,32,16]{1,2,0:T(8,128)S(1)} %convolution_bitcast_fusion), channel_id=2, replica_groups=mesh['groups'=2,'rows'=4,'cols'=2,'sub'=2] {'cols','sub'}, dimensions={0}, use_global_device_ids=true | all-gather | bytes 40960 | tf_op jit(solution)/shard_map/all_gather | solution.py:48
  50.8 1.6 fusion.9
  52.4 51.4 %all-reduce.4.cloned.1.call-done = f32[4,32,2048]{2,1,0:T(8,128)} async-done(((f32[4,32,2048]{2,1,0:T(8,128)}), f32[4,32,2048]{2,1,0:T(8,128)}) %all-reduce.4.cloned.1.call-update) | async-done | bytes 1048592 | tf_op jit(solution)/shard_map/psum | solution.py:51
  103.9 2.7 fusion.10
  106.6 11.8 %psum.59 = f32[4,32,32]{1,2,0:T(8,128)S(1)} all-reduce(f32[4,32,32]{1,2,0:T(8,128)S(1)} %fusion.10), channel_id=1, replica_groups=mesh['groups'=2,'rows'=4,'cols'=2,'sub'=2] {'cols','sub'}, use_global_device_ids=true, to_apply=%region_6.0 | all-reduce | flops 4096 | bytes 32768 | tf_op jit(solution)/shard_map/psum | solution.py:52
  118.6 11.7 %custom-call.10 = f32[4,32,32]{2,1,0:T(8,128)S(1)} custom-call(f32[4,32,32]{2,1,0:T(8,128)S(1)} %fusion.8), custom_call_target="Cholesky" | custom-call | tf_op jit(solution)/shard_map/jit(cholesky)/cholesky | solution.py:25
  130.5 9.8 %custom-call.11 = f32[4,1,32,32]{2,3,1,0:T(8,128)S(1)} custom-call(f32[4,1,32,32]{3,2,1,0:T(8,128)S(1)} %select_bitcast_fusion.2), custom_call_target="InvertDiagBlocksLowerTriangular" | custom-call | tf_op jit(solution)/shard_map/jit(_solve_triangular)/vmap()/triangular_solve | solution.py:26
  141.7 5.4 %all-gather.1 = f32[16,32,16]{1,2,0:T(8,128)S(1)} all-gather(f32[4,32,16]{1,2,0:T(8,128)S(1)} %fusion.11), channel_id=3, replica_groups=mesh['groups'=2,'rows'=4,'cols'=2,'sub'=2] {'cols','sub'}, dimensions={0}, use_global_device_ids=true | all-gather | bytes 40960 | tf_op jit(solution)/shard_map/all_gather | solution.py:48
  147.2 1.6 fusion.12
  148.8 50.4 %all-reduce.6.cloned.1.call-done = f32[4,32,2048]{2,1,0:T(8,128)} async-done(((f32[4,32,2048]{2,1,0:T(8,128)}), f32[4,32,2048]{2,1,0:T(8,128)}) %all-reduce.6.cloned.1.call-update) | async-done | bytes 1048592 | tf_op jit(solution)/shard_map/psum | solution.py:51
  199.2 2.7 fusion.13
  201.9 11.8 %psum.61 = f32[4,32,32]{1,2,0:T(8,128)S(1)} all-reduce(f32[4,32,32]{1,2,0:T(8,128)S(1)} %fusion.13), channel_id=1, replica_groups=mesh['groups'=2,'rows'=4,'cols'=2,'sub'=2] {'cols','sub'}, use_global_device_ids=true, to_apply=%region_11.0 | all-reduce | flops 4096 | bytes 32768 | tf_op jit(solution)/shard_map/psum | solution.py:52
  213.9 11.7 %custom-call.12 = f32[4,32,32]{2,1,0:T(8,128)S(1)} custom-call(f32[4,32,32]{2,1,0:T(8,128)S(1)} %fusion.6), custom_call_target="Cholesky" | custom-call | tf_op jit(solution)/shard_map/jit(cholesky)/cholesky | solution.py:25
  225.9 9.8 %custom-call.13 = f32[4,1,32,32]{2,3,1,0:T(8,128)S(1)} custom-call(f32[4,1,32,32]{3,2,1,0:T(8,128)S(1)} %select_bitcast_fusion.1), custom_call_target="InvertDiagBlocksLowerTriangular" | custom-call | tf_op jit(solution)/shard_map/jit(_solve_triangular)/vmap()/triangular_solve | solution.py:26
  237.0 5.4 %all-gather.2 = f32[16,32,16]{1,2,0:T(8,128)S(1)} all-gather(f32[4,32,16]{1,2,0:T(8,128)S(1)} %fusion.14), channel_id=4, replica_groups=mesh['groups'=2,'rows'=4,'cols'=2,'sub'=2] {'cols','sub'}, dimensions={0}, use_global_device_ids=true | all-gather | bytes 40960 | tf_op jit(solution)/shard_map/all_gather | solution.py:48
  242.5 1.6 fusion.15
  244.1 50.4 %all-reduce.8.cloned.1.call-done = f32[4,32,2048]{2,1,0:T(8,128)} async-done(((f32[4,32,2048]{2,1,0:T(8,128)}), f32[4,32,2048]{2,1,0:T(8,128)}) %all-reduce.8.cloned.1.call-update) | async-done | bytes 1048592 | tf_op jit(solution)/shard_map/psum | solution.py:51
  294.5 2.7 fusion.16
  297.3 11.8 %psum.63 = f32[4,32,32]{1,2,0:T(8,128)S(1)} all-reduce(f32[4,32,32]{1,2,0:T(8,128)S(1)} %fusion.16), channel_id=1, replica_groups=mesh['groups'=2,'rows'=4,'cols'=2,'sub'=2] {'cols','sub'}, use_global_device_ids=true, to_apply=%region_14.17 | all-reduce | flops 4096 | bytes 32768 | tf_op jit(solution)/shard_map/psum | solution.py:52
  309.2 11.7 %custom-call.14 = f32[4,32,32]{2,1,0:T(8,128)S(1)} custom-call(f32[4,32,32]{2,1,0:T(8,128)S(1)} %fusion.4), custom_call_target="Cholesky" | custom-call | tf_op jit(solution)/shard_map/jit(cholesky)/cholesky | solution.py:25
  321.2 9.8 %custom-call.15 = f32[4,1,32,32]{2,3,1,0:T(8,128)S(1)} custom-call(f32[4,1,32,32]{3,2,1,0:T(8,128)S(1)} %select_bitcast_fusion), custom_call_target="InvertDiagBlocksLowerTriangular" | custom-call | tf_op jit(solution)/shard_map/jit(_solve_triangular)/vmap()/triangular_solve | solution.py:26
  331.0 2.0 fusion.2
  (52 shorter events, 5.8 us)
Async XLA Ops:
  6.5 22.3 %copy-start.3 = (f32[4,16,2048]{2,1,0:T(8,128)S(1)}, f32[4,16,2048]{2,1,0:T(8,128)}, u32[]{:S(2)}) copy-start(f32[4,16,2048]{2,1,0:T(8,128)} %param.6) | copy-start | bytes 1572868
  6.5 97.3 %all-reduce.4.cloned.1.call-start = ((), (), s32[]{:S(2)}) async-start(), calls=%async_computation | async-start | bytes 2097152 | tf_op jit(solution)/shard_map/psum | solution.py:51
  6.5 22.3 %copy-start.5 = (s32[4,2048]{1,0:T(4,128)S(1)}, s32[4,2048]{1,0:T(4,128)}, u32[]{:S(2)}) copy-start(s32[4,2048]{1,0:T(4,128)} %param.7) | copy-start | bytes 98308
  7.8 37.2 %copy-start.4 = (f32[4,32,2048]{2,1,0:T(8,128)S(1)}, f32[4,32,2048]{2,1,0:T(8,128)}, u32[]{:S(2)}) copy-start(f32[4,32,2048]{2,1,0:T(8,128)} %param.8) | copy-start | bytes 3145732
  52.4 146.8 %all-reduce.6.cloned.1.call-start = ((), (), s32[]{:S(2)}) async-start(), calls=%async_computation.1 | async-start | bytes 2097152 | tf_op jit(solution)/shard_map/psum | solution.py:51
  103.9 36.5 %copy-start = (f32[4,32,2048]{2,1,0:T(8,128)S(1)}, f32[4,32,2048]{2,1,0:T(8,128)}, u32[]{:S(2)}) copy-start(f32[4,32,2048]{2,1,0:T(8,128)} %all-reduce.4.cloned.1.call-done) | copy-start | bytes 3145732
  148.8 145.7 %all-reduce.8.cloned.1.call-start = ((), (), s32[]{:S(2)}) async-start(), calls=%async_computation.2 | async-start | bytes 2097152 | tf_op jit(solution)/shard_map/psum | solution.py:51
  199.2 36.5 %copy-start.1 = (f32[4,32,2048]{2,1,0:T(8,128)S(1)}, f32[4,32,2048]{2,1,0:T(8,128)}, u32[]{:S(2)}) copy-start(f32[4,32,2048]{2,1,0:T(8,128)} %all-reduce.6.cloned.1.call-done) | copy-start | bytes 3145732
  294.5 36.5 %copy-start.2 = (f32[4,32,2048]{2,1,0:T(8,128)S(1)}, f32[4,32,2048]{2,1,0:T(8,128)}, u32[]{:S(2)}) copy-start(f32[4,32,2048]{2,1,0:T(8,128)} %all-reduce.8.cloned.1.call-done) | copy-start | bytes 3145732
Sparse Core Ops, SparseCore 0:
  52.5 51.3 all-reduce.3
  148.9 50.2 all-reduce.5
  244.2 50.2 all-reduce.7
